TPU v7x, 32 devices: a whole 2x2x4 slice. The times are simulated.
32 devices in a mesh: dp: 8 (over y, x, core), mp: 4 (over z).
Axes of the slice: x: 2, y: 2, z: 4, core: 2. Of those that a mesh axis runs over, the one named last changes fastest.
Arguments:
- tokens: bfloat16 [5120, 768], P('dp'), may hold values from -6 to 6
- segment_ids: int32 [8, 640], P('dp'), may hold values from 0 to 3, never falling along the last dimension, each value on 1 to 320 neighbouring positions
- token_types: int32 [8, 640], P('dp'), may hold values 0 or 1
- q_weight: bfloat16 [4, 768, 768], P(None, None, 'mp'), may hold values from -0.21875 to 0.21875
- k_weight: bfloat16 [768, 768], P(None, 'mp'), may hold values from -0.21875 to 0.21875
- v_weight: bfloat16 [768, 768], P(None, 'mp'), may hold values from -0.21875 to 0.21875
- o_weight: bfloat16 [768, 768], P('mp'), may hold values from -2.5 to 2.5
- o_bias: float32 [768], replicated, may hold values from -1.5 to 1.5
- norm1_gain: float32 [768], replicated, may hold values from 0.25 to 1.75
- norm1_shift: float32 [768], replicated, may hold values from -1.5 to 1.5
- in_weight: bfloat16 [768, 3072], P(None, 'mp'), may hold values from -0.21875 to 0.21875
- in_bias: float32 [3072], P('mp'), may hold values from -1.5 to 1.5
- out_weight: bfloat16 [3072, 768], P('mp'), may hold values from -0.109375 to 0.109375
- out_bias: float32 [768], replicated, may hold values from -1.5 to 1.5
- norm2_gain: float32 [768], replicated, may hold values from 0.25 to 1.75
- norm2_shift: float32 [768], replicated, may hold values from -1.5 to 1.5
- cotangent: bfloat16 [5120, 768], P('dp'), may hold values from -6 to 6
Outputs:
- layer_out: bfloat16 [5120, 768], P('dp')
- tokens_grad: bfloat16 [5120, 768], P('dp')
- q_grad: float32 [4, 768, 768], P(None, 'dp', 'mp')
- k_grad: float32 [768, 768], P('dp', 'mp')
- v_grad: float32 [768, 768], P('dp', 'mp')
- o_grad: float32 [768, 768], P('mp', 'dp')
- o_bias_grad: float32 [768], replicated
- norm1_gain_grad: float32 [768], replicated
- norm1_shift_grad: float32 [768], replicated
- in_grad: float32 [768, 3072], P('dp', 'mp')
- in_bias_grad: float32 [3072], P('mp')
- out_grad: float32 [3072, 768], P('mp', 'dp')
- out_bias_grad: float32 [768], replicated
- norm2_gain_grad: float32 [768], replicated
- norm2_shift_grad: float32 [768], replicated
Inputs may be any that keep to these rules, and one draw needn't show every extreme that they name: `segment_ids`: a sequence's rows with equal ids form one run.
All inputs are finite; a program needn't handle non-finite values. No bound on the sum of `token_types` on one device may be relied on, other than what follows from the above.
Results may differ from a plain program's by a relative error of at most 0.019.
Values may be sent and summed in bfloat16 or wider, within the bound.
A program may use at most 128 MiB of HBM per device.

v0:
```python
import jax
import jax.numpy as jnp
from jax import lax
from jax.sharding import PartitionSpec as P

HD = 64
norm_epsilon = 1e-05


def layer_norm(inputs, gain, shift):
    average = jnp.mean(inputs, axis=-1, keepdims=True)
    centred = inputs - average
    spread = jnp.mean(centred * centred, axis=-1, keepdims=True)
    return centred * lax.rsqrt(spread + norm_epsilon) * gain + shift


def gelu_exact(inputs):
    return jax.nn.gelu(inputs, approximate=False)


def matmul(left, right):
    return jnp.dot(left, right, preferred_element_type=jnp.float32)


def local(
    tokens,
    segment_ids,
    token_types,
    q_weight,
    k_weight,
    v_weight,
    o_weight,
    o_bias,
    norm1_gain,
    norm1_shift,
    in_weight,
    in_bias,
    out_weight,
    out_bias,
    norm2_gain,
    norm2_shift,
    cotangent,
):
    row_count = tokens.shape[0]
    groups, length = segment_ids.shape
    local_width = k_weight.shape[1]
    head_count = local_width // HD
    score_scale = HD ** (-0.5)
    entity = token_types == 1
    chooser = entity[:, :, None, None]
    key_entity = entity[:, None, None, :]
    same_doc = (segment_ids[:, :, None] == segment_ids[:, None, :])[:, None]
    share_rows = row_count // lax.axis_size("mp")
    row_offset = lax.axis_index("mp") * share_rows
    queries = jnp.einsum(
        "rd,tdc->trc", tokens, q_weight, preferred_element_type=jnp.float32
    ).astype(jnp.bfloat16)
    keys = matmul(tokens, k_weight).astype(jnp.bfloat16)
    values = matmul(tokens, v_weight).astype(jnp.bfloat16)
    query_four = queries.reshape(4, groups, length, head_count, HD)
    query_word = jnp.where(chooser, query_four[2], query_four[0])
    query_ent = jnp.where(chooser, query_four[3], query_four[1])
    key_heads = keys.reshape(groups, length, head_count, HD)
    value_heads = values.reshape(groups, length, head_count, HD)

    def scores_now():
        raw_word = jnp.einsum(
            "gqhc,gkhc->ghqk", query_word, key_heads, preferred_element_type=jnp.float32
        )
        raw_ent = jnp.einsum(
            "gqhc,gkhc->ghqk", query_ent, key_heads, preferred_element_type=jnp.float32
        )
        raw_all = jnp.where(key_entity, raw_ent, raw_word)
        return jnp.where(same_doc, raw_all * score_scale, -1000000000.0)

    scores = scores_now()
    highest = jnp.max(scores, axis=-1, keepdims=True)
    log_total = highest + jnp.log(jnp.sum(jnp.exp(scores - highest), axis=-1, keepdims=True))
    attention_low = jnp.exp(scores - log_total).astype(jnp.bfloat16)
    mixed = jnp.einsum(
        "ghqk,gkhc->gqhc", attention_low, value_heads, preferred_element_type=jnp.float32
    )
    mixed = mixed.reshape(row_count, local_width).astype(jnp.bfloat16)
    token_wide = tokens.astype(jnp.float32)
    branch = lax.psum(matmul(mixed, o_weight), "mp") + o_bias
    hidden, norm1_pull = jax.vjp(layer_norm, token_wide + branch, norm1_gain, norm1_shift)
    hidden_low = hidden.astype(jnp.bfloat16)
    inner_pre = matmul(hidden_low, in_weight) + in_bias
    activated, gelu_pull = jax.vjp(gelu_exact, inner_pre)
    activated_low = activated.astype(jnp.bfloat16)
    ffn_out = (
        lax.psum(matmul(activated_low, out_weight).astype(jnp.bfloat16), "mp").astype(jnp.float32)
        + out_bias
    )
    result, norm2_pull = jax.vjp(layer_norm, hidden + ffn_out, norm2_gain, norm2_shift)
    layer_out = result.astype(jnp.bfloat16)
    d_res2, d_gain2, d_shift2 = norm2_pull(cotangent.astype(jnp.float32))
    d_out_bias = jnp.sum(d_res2, axis=0)
    grad_ffn = d_res2.astype(jnp.bfloat16)
    d_out_weight = matmul(activated_low.T, grad_ffn)
    (d_inner,) = gelu_pull(matmul(grad_ffn, out_weight.T))
    d_in_bias = jnp.sum(d_inner, axis=0)
    inner_low = d_inner.astype(jnp.bfloat16)
    d_in_weight = matmul(hidden_low.T, inner_low)
    d_hidden = d_res2 + lax.psum(matmul(inner_low, in_weight.T).astype(jnp.bfloat16), "mp").astype(
        jnp.float32
    )
    d_res1, d_gain1, d_shift1 = norm1_pull(d_hidden)
    d_o_bias = jnp.sum(d_res1, axis=0)
    grad_branch = d_res1.astype(jnp.bfloat16)
    d_o_weight = matmul(mixed.T, grad_branch)
    d_mixed = matmul(grad_branch, o_weight.T).astype(jnp.bfloat16)
    mixed_heads = d_mixed.reshape(groups, length, head_count, HD)
    attention = jnp.exp(scores_now() - log_total)
    d_probs = jnp.einsum(
        "gqhc,gkhc->ghqk", mixed_heads, value_heads, preferred_element_type=jnp.float32
    )
    d_values = jnp.einsum(
        "ghqk,gqhc->gkhc",
        attention.astype(jnp.bfloat16),
        mixed_heads,
        preferred_element_type=jnp.float32,
    )
    row_delta = jnp.sum(attention * d_probs, axis=-1, keepdims=True)
    d_raw = (attention * (d_probs - row_delta) * score_scale).astype(jnp.bfloat16)
    nothing = jnp.zeros_like(d_raw)
    raw_word = jnp.where(key_entity, nothing, d_raw)
    raw_ent = jnp.where(key_entity, d_raw, nothing)
    d_query_word = jnp.einsum(
        "ghqk,gkhc->gqhc", raw_word, key_heads, preferred_element_type=jnp.float32
    )
    d_query_ent = jnp.einsum(
        "ghqk,gkhc->gqhc", raw_ent, key_heads, preferred_element_type=jnp.float32
    )
    d_keys = jnp.einsum(
        "ghqk,gqhc->gkhc", raw_word, query_word, preferred_element_type=jnp.float32
    ) + jnp.einsum("ghqk,gqhc->gkhc", raw_ent, query_ent, preferred_element_type=jnp.float32)
    empty_rows = jnp.zeros_like(d_query_word)
    d_queries = (
        jnp.stack(
            [
                jnp.where(chooser, empty_rows, d_query_word),
                jnp.where(chooser, empty_rows, d_query_ent),
                jnp.where(chooser, d_query_word, empty_rows),
                jnp.where(chooser, d_query_ent, empty_rows),
            ]
        )
        .reshape(4, row_count, local_width)
        .astype(jnp.bfloat16)
    )
    d_keys_low = d_keys.reshape(row_count, local_width).astype(jnp.bfloat16)
    d_values_low = d_values.reshape(row_count, local_width).astype(jnp.bfloat16)
    d_q_weight = jnp.einsum("rd,trc->tdc", tokens, d_queries, preferred_element_type=jnp.float32)
    d_k_weight = matmul(tokens.T, d_keys_low)
    d_v_weight = matmul(tokens.T, d_values_low)
    res_rows = lax.dynamic_slice_in_dim(d_res1, row_offset, share_rows, 0)
    total = jnp.einsum("trc,tdc->rd", d_queries, q_weight, preferred_element_type=jnp.float32)
    grad_rows = (
        res_rows
        + lax.psum_scatter(
            (total + matmul(d_keys_low, k_weight.T) + matmul(d_values_low, v_weight.T)).astype(
                jnp.bfloat16
            ),
            "mp",
            scatter_dimension=0,
            tiled=True,
        ).astype(jnp.float32)
    ).astype(jnp.bfloat16)
    tokens_grad = lax.all_gather(grad_rows, "mp", axis=0, tiled=True)
    d_q_weight, d_k_weight, d_v_weight, d_o_weight, d_in_weight, d_out_weight = (
        lax.psum_scatter(d_q_weight, "dp", scatter_dimension=1, tiled=True),
        lax.psum_scatter(d_k_weight, "dp", scatter_dimension=0, tiled=True),
        lax.psum_scatter(d_v_weight, "dp", scatter_dimension=0, tiled=True),
        lax.psum_scatter(d_o_weight, "dp", scatter_dimension=1, tiled=True),
        lax.psum_scatter(d_in_weight, "dp", scatter_dimension=0, tiled=True),
        lax.psum_scatter(d_out_weight, "dp", scatter_dimension=1, tiled=True),
    )
    d_o_bias, d_gain1, d_shift1, d_in_bias, d_out_bias, d_gain2, d_shift2 = lax.psum(
        (d_o_bias, d_gain1, d_shift1, d_in_bias, d_out_bias, d_gain2, d_shift2), "dp"
    )
    return (
        layer_out,
        tokens_grad,
        d_q_weight,
        d_k_weight,
        d_v_weight,
        d_o_weight,
        d_o_bias,
        d_gain1,
        d_shift1,
        d_in_weight,
        d_in_bias,
        d_out_weight,
        d_out_bias,
        d_gain2,
        d_shift2,
    )


def solution(mesh):
    return jax.shard_map(
        local,
        mesh=mesh,
        in_specs=(
            P("dp", None),
            P("dp", None),
            P("dp", None),
            P(None, None, "mp"),
            P(None, "mp"),
            P(None, "mp"),
            P("mp", None),
            P(),
            P(),
            P(),
            P(None, "mp"),
            P("mp"),
            P("mp", None),
            P(),
            P(),
            P(),
            P("dp", None),
        ),
        out_specs=(
            P("dp", None),
            P("dp", None),
            P(None, "dp", "mp"),
            P("dp", "mp"),
            P("dp", "mp"),
            P("mp", "dp"),
            P(),
            P(),
            P(),
            P("dp", "mp"),
            P("mp"),
            P("mp", "dp"),
            P(),
            P(),
            P(),
        ),
        check_vma=False,
    )
```

profile of v0, /device:TPU:0, one launch (start us, length us, event | category | flops | bytes accessed | tf_op | source)
XLA Modules:
  0.0 547.0 jit_solution(5020968630286662695)
XLA Ops:
  22.2 84.7 %all-reduce.5.cloned.1.call-done = f32[640,768]{1,0:T(8,128)} async-done(((f32[640,768]{1,0:T(8,128)}), f32[640,768]{1,0:T(8,128)}) %all-reduce.5.cloned.1.call-update) | async-done | bytes 1966096 | tf_op jit(solution)/shard_map/psum | solution.py:85
  109.7 6.5 %multiply_convert_fusion.1 = (bf16[640,768]{1,0:T(8,128)(2,1)S(1)}, f32[640,768]{1,0:T(8,128)}, f32[640,768]{1,0:T(8,128)}) fusion(f32[768]{0:T(1024)S(1)} %copy-done.36, bf16[768,768]{1,0:T(8,128)(2,1)S(1)} %copy-done, f32[640,768]{1,0:T(8,128)S(1)} %get-tuple-element.70, f32[768]{0:T(1024)S(1)} %copy-done.31, f32[768]{0:T(1024)S(1)} %copy-done.27, ...), kind=kOutput, calls=%fused_computation.32 | convolution fusion | flops 789872640 | bytes 8075264 | tf_op jit(solution)/shard_map/dot_general | solution.py:22
  119.6 48.5 %all-reduce.7.cloned.1.call-done = bf16[640,768]{1,0:T(8,128)(2,1)} async-done(((bf16[640,768]{1,0:T(8,128)(2,1)}), bf16[640,768]{1,0:T(8,128)(2,1)}) %all-reduce.7.cloned.1.call-update) | async-done | bytes 983056 | tf_op jit(solution)/shard_map/psum | solution.py:92
  179.6 49.1 %all-reduce.9.cloned.1.call-done = bf16[640,768]{1,0:T(8,128)(2,1)} async-done(((bf16[640,768]{1,0:T(8,128)(2,1)}), bf16[640,768]{1,0:T(8,128)(2,1)}) %all-reduce.9.cloned.1.call-update) | async-done | bytes 983056 | tf_op jit(solution)/shard_map/psum | solution.py:105
  228.7 3.1 multiply_reduce_fusion.1
  235.9 3.4 convolution_convert_fusion.3
  239.3 3.1 fusion.82
  242.4 9.7 %fusion.21 = f32[3,64,640]{2,1,0:T(8,128)} fusion(pred[640]{0:T(1024)(128)(4,1)S(1)} %compare_reduce_fusion, f32[3,640,640]{1,2,0:T(8,128)} %fusion.82, f32[3,640,640]{1,2,0:T(8,128)} %copy-done.2, f32[3,640]{1,0:T(4,128)S(1)} %log_add_fusion, bf16[640,3,64]{0,2,1:T(8,128)(2,1)S(1)} %bitcast.122, bf16[640,3,64]{0,2,1:T(8,128)(2,1)S(1)} %bitcast.120), kind=kOutput, calls=%fused_computation.69 | convolution fusion | flops 167242240 | bytes 10821760 | tf_op jit(solution)/shard_map/ghqk,gqhc->gkhc/dot_general | solution.py:135
  252.1 9.6 %convolution_bitcast_fusion.4 = bf16[1,3,64,640]{3,2,1,0:T(8,128)(2,1)} fusion(bf16[640,3,64]{0,2,1:T(8,128)(2,1)S(1)} %bitcast.104, pred[640]{0:T(1024)(128)(4,1)S(1)} %compare_reduce_fusion, f32[3,640,640]{1,2,0:T(8,128)} %fusion.82, f32[3,640,640]{1,2,0:T(8,128)} %copy-done.2, f32[3,640]{1,0:T(4,128)S(1)} %log_add_fusion), kind=kOutput, calls=%fused_computation.60 | convolution fusion | flops 167119360 | bytes 10330240 | tf_op jit(solution)/shard_map/ghqk,gkhc->gqhc/dot_general | solution.py:132
  263.7 9.3 %fusion.20 = bf16[3,64,640]{2,1,0:T(8,128)(2,1)S(1)} fusion(f32[3,64,640]{2,1,0:T(8,128)} %fusion.21, pred[640]{0:T(1024)(128)(4,1)S(1)} %compare_reduce_fusion, f32[3,640,640]{1,2,0:T(8,128)} %fusion.82, f32[3,640,640]{1,2,0:T(8,128)} %copy-done.2, f32[3,640]{1,0:T(4,128)S(1)} %log_add_fusion, bf16[640,3,64]{0,2,1:T(8,128)(2,1)} %bitcast.118, ...), kind=kOutput, calls=%fused_computation.63 | convolution fusion | flops 167488000 | bytes 11067520 | tf_op jit(solution)/shard_map/ghqk,gqhc->gkhc/dot_general | solution.py:137
  272.9 9.9 %select_convert_fusion.3 = (bf16[1,3,64,640]{3,2,1,0:T(8,128)(2,1)}, bf16[1,3,64,640]{3,2,1,0:T(8,128)(2,1)}, bf16[1,3,64,640]{3,2,1,0:T(8,128)(2,1)}, bf16[1,3,64,640]{3,2,1,0:T(8,128)(2,1)}) fusion(pred[640]{0:T(1024)(128)(4,1)S(1)} %compare_reduce_fusion, bf16[1,3,64,640]{3,2,1,0:T(8,128)(2,1)} %convolution_bitcast_fusion.4, ...), kind=kOutput, calls=%fused_computation.79 | convolution fusion | flops 167610880 | bytes 11313280 | tf_op jit(solution)/shard_map/ghqk,gkhc->gqhc/dot_general | solution.py:129
  284.5 3.6 fusion.12
  288.2 3.9 convolution_bitcast_fusion
  292.1 4.5 copy.56
  296.6 4.7 reshape.292
  309.6 4.2 fusion.64
  315.0 2.8 fusion.44
  317.8 24.7 %all-reduce = (f32[768]{0:T(1024)}, f32[768]{0:T(1024)}, f32[768]{0:T(1024)}, f32[768]{0:T(1024)}, f32[768]{0:T(1024)}, /*index=5*/f32[768]{0:T(1024)}, f32[768]{0:T(1024)}) all-reduce(f32[768]{0:T(1024)S(1)} %get-tuple-element.59, f32[768]{0:T(1024)S(1)} %get-tuple-element.45, ...), channel_id=1, replica_groups=mesh['dp'=8,'mp'=4] {'dp'}, use_global_device_ids=true, to_apply=%region_20.21 | all-reduce | flops 5376 | bytes 43008 | tf_op jit(solution)/shard_map/psum | solution.py:178
  345.3 19.9 %all_gather.3 = bf16[640,768]{1,0:T(8,128)(2,1)S(1)} all-gather(bf16[160,768]{1,0:T(8,128)(2,1)S(1)} %add_convert_fusion.2), channel_id=1, replica_groups=mesh['dp'=8,'mp'=4] {'mp'}, dimensions={0}, use_global_device_ids=true | all-gather | bytes 1228800 | tf_op jit(solution)/shard_map/all_gather | solution.py:169
  365.2 3.9 reduce-scatter.22.cloned.1.call-done
  371.2 36.6 %reduce-scatter.26.cloned.1.call-done = f32[96,192]{1,0:T(8,128)} async-done(((f32[768,192]{1,0:T(8,128)}), f32[96,192]{1,0:T(8,128)}) %reduce-scatter.26.cloned.1.call-update) | async-done | bytes 73744
  407.8 38.7 %reduce-scatter.24.cloned.1.call-done = f32[96,192]{1,0:T(8,128)} async-done(((f32[768,192]{1,0:T(8,128)}), f32[96,192]{1,0:T(8,128)}) %reduce-scatter.24.cloned.1.call-update) | async-done | bytes 73744
  446.5 46.3 %reduce-scatter.20.cloned.1.call-done = f32[768,96]{0,1:T(8,128)} async-done(((f32[768,768]{0,1:T(8,128)}), f32[768,96]{0,1:T(8,128)}) %reduce-scatter.20.cloned.1.call-update) | async-done | bytes 294928 | tf_op jit(solution)/shard_map/reduce_scatter | solution.py:176
  492.8 46.1 %reduce-scatter.18.cloned.1.call-done = f32[96,768]{1,0:T(8,128)} async-done(((f32[768,768]{1,0:T(8,128)}), f32[96,768]{1,0:T(8,128)}) %reduce-scatter.18.cloned.1.call-update) | async-done | bytes 294928 | tf_op jit(solution)/shard_map/reduce_scatter | solution.py:175
  (157 shorter events, 55.3 us)
Async XLA Ops:
  7.2 102.2 %copy-start = (bf16[768,768]{1,0:T(8,128)(2,1)S(1)}, bf16[768,768]{1,0:T(8,128)(2,1)}, u32[]{:S(2)}) copy-start(bf16[768,768]{1,0:T(8,128)(2,1)} %param.27) | copy-start | bytes 3538948
  7.2 4.8 copy-start.3
  7.2 4.5 copy-start.33
  7.2 99.6 %all-reduce.5.cloned.1.call-start = ((), (), s32[]{:S(2)}) async-start(), calls=%async_computation.7 | async-start | bytes 3932160 | tf_op jit(solution)/shard_map/psum | solution.py:85
  9.8 5.6 %copy-start.10 = (bf16[640,192]{0,1:T(8,128)(2,1)}, bf16[640,192]{0,1:T(8,128)(2,1)S(1)}, u32[]{:S(2)}) copy-start(bf16[640,192]{0,1:T(8,128)(2,1)S(1)} %convolution_convert_fusion.6) | copy-start | bytes 737284
  11.7 6.1 %copy-start.12 = (bf16[640,192]{0,1:T(8,128)(2,1)}, bf16[640,192]{0,1:T(8,128)(2,1)S(1)}, u32[]{:S(2)}) copy-start(bf16[640,192]{0,1:T(8,128)(2,1)S(1)} %convolution_convert_fusion.7) | copy-start | bytes 737284
  20.3 86.6 %copy-start.29 = (f32[768]{0:T(1024)S(1)}, f32[768]{0:T(1024)}, u32[]{:S(2)}) copy-start(f32[768]{0:T(1024)} %param.24) | copy-start | bytes 9220
  22.1 146.0 %all-reduce.7.cloned.1.call-start = ((), (), s32[]{:S(2)}) async-start(), calls=%async_computation.8 | async-start | bytes 1966080 | tf_op jit(solution)/shard_map/psum | solution.py:92
  109.7 7.5 %copy-start.34 = (bf16[768,768]{1,0:T(8,128)(2,1)S(1)}, bf16[768,768]{1,0:T(8,128)(2,1)}, u32[]{:S(2)}) copy-start(bf16[768,768]{1,0:T(8,128)(2,1)} %param.29) | copy-start | bytes 3538948
  117.2 50.9 %copy-start.30 = (f32[768]{0:T(1024)S(1)}, f32[768]{0:T(1024)}, u32[]{:S(2)}) copy-start(f32[768]{0:T(1024)} %param.30) | copy-start | bytes 9220
  119.1 109.6 %all-reduce.9.cloned.1.call-start = ((), (), s32[]{:S(2)}) async-start(), calls=%async_computation.9 | async-start | bytes 1966080 | tf_op jit(solution)/shard_map/psum | solution.py:105
  179.5 163.0 %reduce-scatter.28.cloned.1.call-start = ((), (), s32[]{:S(2)}) async-start(), calls=%async_computation.16 | async-start | bytes 884736
  242.4 9.7 %copy-start.11 = (bf16[640,192]{0,1:T(8,128)(2,1)S(1)}, bf16[640,192]{0,1:T(8,128)(2,1)}, u32[]{:S(2)}) copy-start(bf16[640,192]{0,1:T(8,128)(2,1)} %copy-done.10) | copy-start | bytes 737284
  252.1 9.8 %copy-start.17 = (bf16[768,192]{0,1:T(8,128)(2,1)S(1)}, bf16[768,192]{0,1:T(8,128)(2,1)}, u32[]{:S(2)}) copy-start(bf16[768,192]{0,1:T(8,128)(2,1)} %param.22) | copy-start | bytes 884740
  261.7 82.4 %reduce-scatter.16.cloned.1.call-start = ((), (), s32[]{:S(2)}) async-start(), calls=%async_computation.10 | async-start | bytes 1228800 | tf_op jit(solution)/shard_map/reduce_scatter | solution.py:160
  272.9 9.9 %copy-start.19 = (bf16[3,64,640]{2,1,0:T(8,128)(2,1)}, bf16[3,64,640]{2,1,0:T(8,128)(2,1)S(1)}, u32[]{:S(2)}) copy-start(bf16[3,64,640]{2,1,0:T(8,128)(2,1)S(1)} %fusion.20) | copy-start | bytes 737284
  272.9 9.9 %copy-start.18 = (bf16[768,192]{0,1:T(8,128)(2,1)S(1)}, bf16[768,192]{0,1:T(8,128)(2,1)}, u32[]{:S(2)}) copy-start(bf16[768,192]{0,1:T(8,128)(2,1)} %param.21) | copy-start | bytes 884740
  284.5 3.7 copy-start.4
  288.1 81.0 %reduce-scatter.22.cloned.1.call-start = ((), (), s32[]{:S(2)}) async-start(), calls=%async_computation.13 | async-start | bytes 2654208
  301.3 106.5 %reduce-scatter.26.cloned.1.call-start = ((), (), s32[]{:S(2)}) async-start(), calls=%async_computation.15 | async-start | bytes 884736
  304.8 141.7 %reduce-scatter.24.cloned.1.call-start = ((), (), s32[]{:S(2)}) async-start(), calls=%async_computation.14 | async-start | bytes 884736
  309.5 183.3 %reduce-scatter.20.cloned.1.call-start = ((), (), s32[]{:S(2)}) async-start(), calls=%async_computation.12 | async-start | bytes 2654208 | tf_op jit(solution)/shard_map/reduce_scatter | solution.py:176
  313.8 225.2 %reduce-scatter.18.cloned.1.call-start = ((), (), s32[]{:S(2)}) async-start(), calls=%async_computation.11 | async-start | bytes 2654208 | tf_op jit(solution)/shard_map/reduce_scatter | solution.py:175
  345.3 194.6 %copy-start.1 = (bf16[768,768]{1,0:T(8,128)(2,1)S(1)}, bf16[768,768]{1,0:T(8,128)(2,1)}, u32[]{:S(2)}) copy-start(bf16[768,768]{1,0:T(8,128)(2,1)} %param.27) | copy-start | bytes 3538948
  (31 other events, 52.7 us)
Sparse Core Ops, SparseCore 0:
  22.2 84.5 all-reduce.4
  119.2 48.8 all-reduce.6
  179.6 49.0 all-reduce.8
  261.8 34.1 reduce-scatter.27
  298.7 26.2 reduce-scatter.15
  328.2 40.9 reduce-scatter.21
  372.9 34.9 reduce-scatter.25
  411.6 34.9 reduce-scatter.23
  450.5 42.3 reduce-scatter.19
  496.6 42.3 reduce-scatter.17
where the time goes:
time: 554 us; the launch traced here: 547 us
  waiting for transfers between devices  354 us (64%)
  matrix products  90 us (16%)
  blocking collectives  44.6 us (8%)
  local copies, waits for them, and re-layouts  27.3 us (5%)
  between operations  14.9 us (3%)
  other arithmetic  14.8 us (3%)
    psum x1, waiting for transfers between devices, local(): branch = lax.psum(matmul(mixed, o_weight), 'mp') + o_bias  84.7 us
    unnamed x14, waiting for transfers between devices  79.4 us
    psum x1, waiting for transfers between devices, local(): lax.psum(matmul(inner_low, in_weight.T).astype(jnp.bfloat16), 'mp')  49.1 us
    psum x1, waiting for transfers between devices, local(): lax.psum(matmul(activated_low, out_weight).astype(jnp.bfloat16), 'mp')  48.5 us
    reduce_scatter x1, waiting for transfers between devices, local(): lax.psum_scatter(d_out_weight, 'dp', scatter_dimension=1, tiled=True)  46.3 us
    reduce_scatter x1, waiting for transfers between devices, local(): lax.psum_scatter(d_in_weight, 'dp', scatter_dimension=0, tiled=True)  46.1 us
    dot_general x14, matrix products, matmul(): return jnp.dot(left, right, preferred_element_type=jnp.float32)  30.4 us
    unnamed x98, local copies, waits for them, and re-layouts  27.2 us
  transfers between devices with their start and end apart: 10, of which 8 were waited for; matrix products, arithmetic and copies ran while one was open for 11% of the time, Pallas kernels for 0%

commit v1 on v0

--- a/solution.py
+++ b/solution.py
@@ -82,7 +82,7 @@
     )
     mixed = mixed.reshape(row_count, local_width).astype(jnp.bfloat16)
     token_wide = tokens.astype(jnp.float32)
-    branch = lax.psum(matmul(mixed, o_weight), "mp") + o_bias
+    branch = jnp.sum(lax.all_gather(matmul(mixed, o_weight), "mp"), axis=0) + o_bias
     hidden, norm1_pull = jax.vjp(layer_norm, token_wide + branch, norm1_gain, norm1_shift)
     hidden_low = hidden.astype(jnp.bfloat16)
     inner_pre = matmul(hidden_low, in_weight) + in_bias

time: 554 us -> 618 us (1.12)
  waiting for transfers between devices: 354 us -> 413 us
    all_gather x0 -> x1, waiting for transfers between devices: none -> 144 us  [local(): lax.all_gather(matmul(mixed, o_weight), 'mp')]
    psum x1 -> x0, waiting for transfers between devices: 84.7 us -> none  [local(): branch = lax.psum(matmul(mixed, o_weight), 'mp') + o_bias]
  transfers between devices with their start and end apart: 10 -> 10, of which waited for: 8 -> 8; matrix products, arithmetic and copies ran while one was open for 11% -> 10% of each run, Pallas kernels for 0% -> 0%
where the time goes in v1:
time: 618 us; the launch traced here: 610 us
  waiting for transfers between devices  413 us (67%)
  matrix products  89.8 us (15%)
  blocking collectives  44.5 us (7%)
  local copies, waits for them, and re-layouts  27.1 us (4%)
  other arithmetic  20.1 us (3%)
  between operations  14.9 us (2%)
    all_gather x1, waiting for transfers between devices, local(): lax.all_gather(matmul(mixed, o_weight), 'mp')  144 us
    unnamed x14, waiting for transfers between devices  79.5 us
    psum x1, waiting for transfers between devices, local(): lax.psum(matmul(inner_low, in_weight.T).astype(jnp.bfloat16), 'mp')  49.1 us
    psum x1, waiting for transfers between devices, local(): lax.psum(matmul(activated_low, out_weight).astype(jnp.bfloat16), 'mp')  47.7 us
    reduce_scatter x1, waiting for transfers between devices, local(): lax.psum_scatter(d_out_weight, 'dp', scatter_dimension=1, tiled=True)  46.3 us
    reduce_scatter x1, waiting for transfers between devices, local(): lax.psum_scatter(d_in_weight, 'dp', scatter_dimension=0, tiled=True)  46.1 us
    dot_general x14, matrix products, matmul(): return jnp.dot(left, right, preferred_element_type=jnp.float32)  30.3 us
    unnamed x98, local copies, waits for them, and re-layouts  27 us
  transfers between devices with their start and end apart: 10, of which 8 were waited for; matrix products, arithmetic and copies ran while one was open for 10% of the time, Pallas kernels for 0%

profile of v1, /device:TPU:0, one launch (start us, length us, event | category | flops | bytes accessed | tf_op | source)
XLA Modules:
  0.0 610.3 jit_solution(2320562929234718520)
XLA Ops:
  22.1 143.9 %all-gather.3.cloned.1.call-done = f32[2560,768]{1,0:T(8,128)} async-done(((f32[640,768]{1,0:T(8,128)}), f32[2560,768]{1,0:T(8,128)}) %all-gather.3.cloned.1.call-update) | async-done | bytes 7864336 | tf_op jit(solution)/shard_map/all_gather | solution.py:85
  166.0 5.3 reduce_sum.160
  174.1 6.5 %multiply_convert_fusion.1 = (bf16[640,768]{1,0:T(8,128)(2,1)S(1)}, f32[640,768]{1,0:T(8,128)}, f32[640,768]{1,0:T(8,128)}) fusion(f32[768]{0:T(1024)S(1)} %copy-done.36, bf16[768,768]{1,0:T(8,128)(2,1)S(1)} %copy-done, f32[640,768]{1,0:T(8,128)S(1)} %get-tuple-element.70, f32[768]{0:T(1024)S(1)} %copy-done.31, f32[768]{0:T(1024)S(1)} %copy-done.27, ...), kind=kOutput, calls=%fused_computation.32 | convolution fusion | flops 789872640 | bytes 8075264 | tf_op jit(solution)/shard_map/dot_general | solution.py:22
  183.9 47.7 %all-reduce.4.cloned.1.call-done = bf16[640,768]{1,0:T(8,128)(2,1)} async-done(((bf16[640,768]{1,0:T(8,128)(2,1)}), bf16[640,768]{1,0:T(8,128)(2,1)}) %all-reduce.4.cloned.1.call-update) | async-done | bytes 983056 | tf_op jit(solution)/shard_map/psum | solution.py:92
  243.0 49.1 %all-reduce.6.cloned.1.call-done = bf16[640,768]{1,0:T(8,128)(2,1)} async-done(((bf16[640,768]{1,0:T(8,128)(2,1)}), bf16[640,768]{1,0:T(8,128)(2,1)}) %all-reduce.6.cloned.1.call-update) | async-done | bytes 983056 | tf_op jit(solution)/shard_map/psum | solution.py:105
  292.2 3.1 multiply_reduce_fusion.1
  299.3 3.4 convolution_convert_fusion.3
  302.7 3.0 fusion.82
  305.7 9.7 %fusion.21 = f32[3,64,640]{2,1,0:T(8,128)} fusion(pred[640]{0:T(1024)(128)(4,1)S(1)} %compare_reduce_fusion, f32[3,640,640]{1,2,0:T(8,128)} %fusion.82, f32[3,640,640]{1,2,0:T(8,128)} %copy-done.2, f32[3,640]{1,0:T(4,128)S(1)} %log_add_fusion, bf16[640,3,64]{0,2,1:T(8,128)(2,1)S(1)} %bitcast.124, bf16[640,3,64]{0,2,1:T(8,128)(2,1)S(1)} %bitcast.122), kind=kOutput, calls=%fused_computation.69 | convolution fusion | flops 167242240 | bytes 10821760 | tf_op jit(solution)/shard_map/ghqk,gqhc->gkhc/dot_general | solution.py:135
  315.4 9.6 %convolution_bitcast_fusion.4 = bf16[1,3,64,640]{3,2,1,0:T(8,128)(2,1)} fusion(bf16[640,3,64]{0,2,1:T(8,128)(2,1)S(1)} %bitcast.106, pred[640]{0:T(1024)(128)(4,1)S(1)} %compare_reduce_fusion, f32[3,640,640]{1,2,0:T(8,128)} %fusion.82, f32[3,640,640]{1,2,0:T(8,128)} %copy-done.2, f32[3,640]{1,0:T(4,128)S(1)} %log_add_fusion), kind=kOutput, calls=%fused_computation.60 | convolution fusion | flops 167119360 | bytes 10330240 | tf_op jit(solution)/shard_map/ghqk,gkhc->gqhc/dot_general | solution.py:132
  327.0 9.3 %fusion.20 = bf16[3,64,640]{2,1,0:T(8,128)(2,1)S(1)} fusion(f32[3,64,640]{2,1,0:T(8,128)} %fusion.21, pred[640]{0:T(1024)(128)(4,1)S(1)} %compare_reduce_fusion, f32[3,640,640]{1,2,0:T(8,128)} %fusion.82, f32[3,640,640]{1,2,0:T(8,128)} %copy-done.2, f32[3,640]{1,0:T(4,128)S(1)} %log_add_fusion, bf16[640,3,64]{0,2,1:T(8,128)(2,1)} %bitcast.120, ...), kind=kOutput, calls=%fused_computation.63 | convolution fusion | flops 167488000 | bytes 11067520 | tf_op jit(solution)/shard_map/ghqk,gqhc->gkhc/dot_general | solution.py:137
  336.3 9.9 %select_convert_fusion.3 = (bf16[1,3,64,640]{3,2,1,0:T(8,128)(2,1)}, bf16[1,3,64,640]{3,2,1,0:T(8,128)(2,1)}, bf16[1,3,64,640]{3,2,1,0:T(8,128)(2,1)}, bf16[1,3,64,640]{3,2,1,0:T(8,128)(2,1)}) fusion(pred[640]{0:T(1024)(128)(4,1)S(1)} %compare_reduce_fusion, bf16[1,3,64,640]{3,2,1,0:T(8,128)(2,1)} %convolution_bitcast_fusion.4, ...), kind=kOutput, calls=%fused_computation.79 | convolution fusion | flops 167610880 | bytes 11313280 | tf_op jit(solution)/shard_map/ghqk,gkhc->gqhc/dot_general | solution.py:129
  347.8 3.6 fusion.12
  351.6 3.9 convolution_bitcast_fusion
  355.4 4.5 copy.56
  359.9 4.7 reshape.293
  372.8 4.2 fusion.64
  381.1 24.7 %all-reduce = (f32[768]{0:T(1024)}, f32[768]{0:T(1024)}, f32[768]{0:T(1024)}, f32[768]{0:T(1024)}, f32[768]{0:T(1024)}, /*index=5*/f32[768]{0:T(1024)}, f32[768]{0:T(1024)}) all-reduce(f32[768]{0:T(1024)S(1)} %get-tuple-element.59, f32[768]{0:T(1024)S(1)} %get-tuple-element.45, ...), channel_id=1, replica_groups=mesh['dp'=8,'mp'=4] {'dp'}, use_global_device_ids=true, to_apply=%region_20.21 | all-reduce | flops 5376 | bytes 43008 | tf_op jit(solution)/shard_map/psum | solution.py:178
  408.6 19.8 %all_gather.11 = bf16[640,768]{1,0:T(8,128)(2,1)S(1)} all-gather(bf16[160,768]{1,0:T(8,128)(2,1)S(1)} %add_convert_fusion.2), channel_id=1, replica_groups=mesh['dp'=8,'mp'=4] {'mp'}, dimensions={0}, use_global_device_ids=true | all-gather | bytes 1228800 | tf_op jit(solution)/shard_map/all_gather | solution.py:169
  428.5 4.0 reduce-scatter.22.cloned.1.call-done
  434.5 36.6 %reduce-scatter.26.cloned.1.call-done = f32[96,192]{1,0:T(8,128)} async-done(((f32[768,192]{1,0:T(8,128)}), f32[96,192]{1,0:T(8,128)}) %reduce-scatter.26.cloned.1.call-update) | async-done | bytes 73744
  471.1 38.7 %reduce-scatter.24.cloned.1.call-done = f32[96,192]{1,0:T(8,128)} async-done(((f32[768,192]{1,0:T(8,128)}), f32[96,192]{1,0:T(8,128)}) %reduce-scatter.24.cloned.1.call-update) | async-done | bytes 73744
  509.8 46.3 %reduce-scatter.20.cloned.1.call-done = f32[768,96]{0,1:T(8,128)} async-done(((f32[768,768]{0,1:T(8,128)}), f32[768,96]{0,1:T(8,128)}) %reduce-scatter.20.cloned.1.call-update) | async-done | bytes 294928 | tf_op jit(solution)/shard_map/reduce_scatter | solution.py:176
  556.2 46.1 %reduce-scatter.18.cloned.1.call-done = f32[96,768]{1,0:T(8,128)} async-done(((f32[768,768]{1,0:T(8,128)}), f32[96,768]{1,0:T(8,128)}) %reduce-scatter.18.cloned.1.call-update) | async-done | bytes 294928 | tf_op jit(solution)/shard_map/reduce_scatter | solution.py:175
  (158 shorter events, 57.8 us)
Async XLA Ops:
  7.2 166.6 %copy-start = (bf16[768,768]{1,0:T(8,128)(2,1)S(1)}, bf16[768,768]{1,0:T(8,128)(2,1)}, u32[]{:S(2)}) copy-start(bf16[768,768]{1,0:T(8,128)(2,1)} %param.27) | copy-start | bytes 3538948
  7.2 4.8 copy-start.3
  7.2 4.5 copy-start.33
  7.2 158.7 %all-gather.3.cloned.1.call-start = ((), (), s32[]{:S(2)}) async-start(), calls=%async_computation.12 | async-start | bytes 9830400 | tf_op jit(solution)/shard_map/all_gather | solution.py:85
  9.8 5.6 copy-start.10
  11.7 6.1 copy-start.12
  22.0 209.6 %all-reduce.4.cloned.1.call-start = ((), (), s32[]{:S(2)}) async-start(), calls=%async_computation.7 | async-start | bytes 1966080 | tf_op jit(solution)/shard_map/psum | solution.py:92
  166.0 5.3 copy-start.29
  174.1 7.4 %copy-start.34 = (bf16[768,768]{1,0:T(8,128)(2,1)S(1)}, bf16[768,768]{1,0:T(8,128)(2,1)}, u32[]{:S(2)}) copy-start(bf16[768,768]{1,0:T(8,128)(2,1)} %param.29) | copy-start | bytes 3538948
  181.5 50.1 %copy-start.30 = (f32[768]{0:T(1024)S(1)}, f32[768]{0:T(1024)}, u32[]{:S(2)}) copy-start(f32[768]{0:T(1024)} %param.30) | copy-start | bytes 9220
  183.4 108.7 %all-reduce.6.cloned.1.call-start = ((), (), s32[]{:S(2)}) async-start(), calls=%async_computation.8 | async-start | bytes 1966080 | tf_op jit(solution)/shard_map/psum | solution.py:105
  243.0 162.8 %reduce-scatter.28.cloned.1.call-start = ((), (), s32[]{:S(2)}) async-start(), calls=%async_computation.16 | async-start | bytes 884736
  305.7 9.7 %copy-start.11 = (bf16[640,192]{0,1:T(8,128)(2,1)S(1)}, bf16[640,192]{0,1:T(8,128)(2,1)}, u32[]{:S(2)}) copy-start(bf16[640,192]{0,1:T(8,128)(2,1)} %copy-done.10) | copy-start | bytes 737284
  315.4 9.8 %copy-start.17 = (bf16[768,192]{0,1:T(8,128)(2,1)S(1)}, bf16[768,192]{0,1:T(8,128)(2,1)}, u32[]{:S(2)}) copy-start(bf16[768,192]{0,1:T(8,128)(2,1)} %param.22) | copy-start | bytes 884740
  325.0 82.4 %reduce-scatter.16.cloned.1.call-start = ((), (), s32[]{:S(2)}) async-start(), calls=%async_computation.9 | async-start | bytes 1228800 | tf_op jit(solution)/shard_map/reduce_scatter | solution.py:160
  336.3 10.0 %copy-start.19 = (bf16[3,64,640]{2,1,0:T(8,128)(2,1)}, bf16[3,64,640]{2,1,0:T(8,128)(2,1)S(1)}, u32[]{:S(2)}) copy-start(bf16[3,64,640]{2,1,0:T(8,128)(2,1)S(1)} %fusion.20) | copy-start | bytes 737284
  336.3 10.0 %copy-start.18 = (bf16[768,192]{0,1:T(8,128)(2,1)S(1)}, bf16[768,192]{0,1:T(8,128)(2,1)}, u32[]{:S(2)}) copy-start(bf16[768,192]{0,1:T(8,128)(2,1)} %param.21) | copy-start | bytes 884740
  347.8 3.7 copy-start.4
  351.5 80.9 %reduce-scatter.22.cloned.1.call-start = ((), (), s32[]{:S(2)}) async-start(), calls=%async_computation.13 | async-start | bytes 2654208
  364.7 106.4 %reduce-scatter.26.cloned.1.call-start = ((), (), s32[]{:S(2)}) async-start(), calls=%async_computation.15 | async-start | bytes 884736
  368.2 141.6 %reduce-scatter.24.cloned.1.call-start = ((), (), s32[]{:S(2)}) async-start(), calls=%async_computation.14 | async-start | bytes 884736
  372.8 183.4 %reduce-scatter.20.cloned.1.call-start = ((), (), s32[]{:S(2)}) async-start(), calls=%async_computation.11 | async-start | bytes 2654208 | tf_op jit(solution)/shard_map/reduce_scatter | solution.py:176
  377.1 225.2 %reduce-scatter.18.cloned.1.call-start = ((), (), s32[]{:S(2)}) async-start(), calls=%async_computation.10 | async-start | bytes 2654208 | tf_op jit(solution)/shard_map/reduce_scatter | solution.py:175
  408.6 194.6 %copy-start.1 = (bf16[768,768]{1,0:T(8,128)(2,1)S(1)}, bf16[768,768]{1,0:T(8,128)(2,1)}, u32[]{:S(2)}) copy-start(bf16[768,768]{1,0:T(8,128)(2,1)} %param.27) | copy-start | bytes 3538948
  (31 other events, 52.4 us)
Sparse Core Ops, SparseCore 0:
  22.2 143.7 all-gather.2
  183.5 48.0 all-reduce.3
  243.1 49.0 all-reduce.5
  325.1 34.1 reduce-scatter.27
  362.0 26.2 reduce-scatter.15
  391.5 40.8 reduce-scatter.21
  436.2 34.9 reduce-scatter.25
  474.8 34.9 reduce-scatter.23
  513.8 42.3 reduce-scatter.19
  559.9 42.3 reduce-scatter.17
